TPU v7x, 32 devices: a 4x4x1 block of a 4x4x8 slice. The times are simulated.
32 devices in a mesh: dp: 1 (over z), sp: 32 (over y, x, core).
Axes of the slice: x: 4, y: 4, z: 1, core: 2. Of those that a mesh axis runs over, the one named last changes fastest.
The devices are a block of a 4x4x8 slice.
Arguments:
- hidden: bfloat16 [2, 12288, 2048], P('dp', 'sp')
- w_in: bfloat16 [2048, 6144], replicated
- w_gate: bfloat16 [2048, 4], replicated
- gate_bias: float32 [4], replicated
- a_log: float32 [4], replicated
- norm_w: float32 [2048], replicated
- w_out: bfloat16 [2048, 2048], replicated
Outputs:
- output: bfloat16 [2, 12288, 2048], P('dp', 'sp')
All inputs are finite; a program needn't handle non-finite values.
Results may differ from a plain program's by a relative error of at most 0.0109516.
Values are sent between devices in bfloat16 or wider.
A program may use at most 768 MiB of HBM per device.

v0:
```python
import jax
import jax.numpy as jnp
from jax import lax
from jax.sharding import PartitionSpec as P

CHUNK = 64
NORM_EPS = 1e-6


def local_parts(x_loc, w_in, w_gate, gate_bias, a_log, val_dim):
    n_rows, seq_len, _ = x_loc.shape
    n_heads = w_gate.shape[1]
    n_chunks = seq_len // CHUNK
    key_dim = (w_in.shape[1] - 2 * val_dim) // 2
    head_k = key_dim // n_heads
    head_v = val_dim // n_heads
    proj_all = jnp.einsum('mtd,dc->mtc', x_loc, w_in, preferred_element_type=jnp.float32).astype(jnp.bfloat16)
    gate_logit = jnp.einsum('mtd,dh->mth', x_loc, w_gate, preferred_element_type=jnp.float32) + gate_bias
    log_decay = -jnp.exp(a_log) * jax.nn.softplus(gate_logit)
    queries = proj_all[:, :, :key_dim].reshape(n_rows, n_chunks, CHUNK, n_heads, head_k)
    key_vecs = proj_all[:, :, key_dim:2 * key_dim].reshape(n_rows, n_chunks, CHUNK, n_heads, head_k)
    values = proj_all[:, :, 2 * key_dim:2 * key_dim + val_dim].reshape(n_rows, n_chunks, CHUNK, n_heads, head_v)
    z_gate = proj_all[:, :, 2 * key_dim + val_dim:]
    cum_in = jnp.cumsum(log_decay.reshape(n_rows, n_chunks, CHUNK, n_heads), axis=2)
    cum_head = jnp.swapaxes(cum_in, 2, 3)
    positions = jnp.arange(CHUNK)
    causal = positions[:, None] >= positions[None, :]
    log_gap = cum_head[..., :, None] - cum_head[..., None, :]
    decay_in = jnp.where(causal, jnp.exp(jnp.where(causal, log_gap, 0.0)), 0.0)
    scores = jnp.einsum('mcihd,mcjhd->mchij', queries, key_vecs, preferred_element_type=jnp.float32) * decay_in
    intra_term = jnp.einsum('mchij,mcjhe->mcihe', scores, values, preferred_element_type=jnp.float32)
    chunk_tot = cum_in[:, :, -1, :]
    chunk_end = jnp.cumsum(chunk_tot, axis=1)
    chunk_start = chunk_end - chunk_tot
    tail_decay = jnp.exp(chunk_tot[:, :, None, :] - cum_in)
    chunk_state = jnp.einsum('mcjhd,mcjhe->mchde', key_vecs * tail_decay[..., None], values, preferred_element_type=jnp.float32)
    chunk_ids = jnp.arange(n_chunks)
    before = (chunk_ids[:, None] > chunk_ids[None, :])[None, :, :, None]
    pass_gap = chunk_start[:, :, None, :] - chunk_end[:, None, :, :]
    pass_weight = jnp.where(before, jnp.exp(jnp.where(before, pass_gap, 0.0)), 0.0)
    start_state = jnp.einsum('mcbh,mbhde->mchde', pass_weight, chunk_state)
    shard_tot = chunk_end[:, -1, :]
    local_state = jnp.einsum('mbh,mbhde->mhde', jnp.exp(shard_tot[:, None, :] - chunk_end), chunk_state)
    return queries, z_gate, intra_term, cum_in, chunk_start, start_state, shard_tot, local_state


def finish(queries, z_gate, intra_term, cum_in, chunk_start, start_state, state_in, norm_w, w_out):
    n_rows, n_chunks, _, n_heads, head_k = queries.shape
    head_v = intra_term.shape[-1]
    full_state = start_state + jnp.exp(chunk_start)[..., None, None] * state_in[:, None]
    inter_term = jnp.einsum('mcihd,mchde->mcihe', queries, full_state, preferred_element_type=jnp.float32) * jnp.exp(cum_in)[..., None]
    attn_out = ((intra_term + inter_term) * head_k ** -0.5).reshape(n_rows, n_chunks * CHUNK, n_heads, head_v)
    normed = attn_out * lax.rsqrt(jnp.mean(attn_out * attn_out, axis=-1, keepdims=True) + NORM_EPS) * norm_w.reshape(n_heads, head_v)
    gated_out = normed.reshape(n_rows, n_chunks * CHUNK, n_heads * head_v) * jax.nn.silu(z_gate.astype(jnp.float32))
    return jnp.einsum('mtc,cd->mtd', gated_out.astype(jnp.bfloat16), w_out, preferred_element_type=jnp.float32).astype(jnp.bfloat16)


def incoming_state(shard_tot, local_state, seq_size):
    shift_pairs = [(source, source + 1) for source in range(seq_size - 1)]
    acc_decay = lax.ppermute(shard_tot, 'sp', shift_pairs)
    acc_state = lax.ppermute(local_state, 'sp', shift_pairs)
    offset = 1
    while offset < seq_size:
        send_pairs = [(source, source + offset) for source in range(seq_size - offset)]
        prev_decay = lax.ppermute(acc_decay, 'sp', send_pairs)
        prev_state = lax.ppermute(acc_state, 'sp', send_pairs)
        acc_state = acc_state + jnp.exp(acc_decay)[:, :, None, None] * prev_state
        acc_decay = acc_decay + prev_decay
        offset = offset * 2
    return acc_state


def solution(mesh):
    seq_size = mesh.shape['sp']

    def device_body(x_loc, w_in, w_gate, gate_bias, a_log, norm_w, w_out):
        queries, z_gate, intra_term, cum_in, chunk_start, start_state, shard_tot, local_state = local_parts(x_loc, w_in, w_gate, gate_bias, a_log, w_out.shape[0])
        state_in = incoming_state(shard_tot, local_state, seq_size)
        return finish(queries, z_gate, intra_term, cum_in, chunk_start, start_state, state_in, norm_w, w_out)

    return jax.shard_map(device_body, mesh=mesh, in_specs=(P('dp', 'sp', None), P(), P(), P(), P(), P(), P()), out_specs=P('dp', 'sp', None), check_vma=False)
```

profile of v0, /device:TPU:110, one launch (start us, length us, event | category | flops | bytes accessed | tf_op | source)
XLA Modules:
  0.0 681.4 jit_solution(4267234245614032995)
XLA Ops:
  6.4 22.9 %fusion.8 = bf16[2,384,6144]{2,1,0:T(8,128)(2,1)S(1)} fusion(bf16[2,384,2048]{2,1,0:T(8,128)(2,1)S(1)} %copy-done, bf16[2048,6144]{1,0:T(8,128)(2,1)} %param.8), kind=kOutput, calls=%fused_computation.9 | convolution fusion | flops 19332071424 | bytes 37748736 | tf_op jit(solution)/shard_map/mtd,dc->mtc/dot_general | solution.py:17
  36.7 4.8 reshape.78
  47.1 12.3 %fusion.27 = bf16[2,6,4,256,512]{4,3,2,1,0:T(8,128)(2,1)} fusion(bf16[2,6,64,4,512]{4,3,2,1,0:T(4,128)(2,1)S(1)} %reshape.78, f32[2,6,64,4]{2,3,1,0:T(4,128)} %copy.89, bf16[2,6,64,4,256]{4,3,2,1,0:T(4,128)(2,1)} %reshape.80), kind=kOutput, calls=%fused_computation.33 | convolution fusion | flops 806879232 | bytes 17313792 | tf_op jit(solution)/shard_map/mcjhd,mcjhe->mchde/dot_general | solution.py:36
  59.5 27.1 %fusion = f32[2,4,1,256,512]{4,2,3,1,0:T(1,128)S(1)} fusion(f32[2,6,4,1,1]{1,3,4,2,0:T(1,128)S(1)} %bitcast.60, bf16[2,6,4,256,512]{4,3,2,1,0:T(8,128)(2,1)} %fusion.27), kind=kOutput, calls=%fused_computation | convolution fusion | flops 12582912 | bytes 16777408 | tf_op jit(solution)/shard_map/mbh,mbhde->mhde/dot_general | solution.py:43
  89.3 47.9 %collective-permute-done = f32[2,4,256,512]{3,2,1,0:T(8,128)S(1)} collective-permute-done((f32[2,4,256,512]{3,2,1,0:T(8,128)S(1)}, f32[2,4,256,512]{3,2,1,0:T(8,128)S(1)}, u32[]{:S(2)}, u32[]{:S(2)}) %collective-permute-start) | collective-permute-done | bytes 4194336 | tf_op jit(solution)/shard_map/ppermute | solution.py:61
  139.1 5.8 collective-permute-start.1
  144.9 42.1 %collective-permute-done.1 = f32[2,4]{1,0:T(2,128)S(1)} collective-permute-done((f32[2,4]{1,0:T(2,128)S(1)}, f32[2,4]{1,0:T(2,128)S(1)}, u32[]{:S(2)}, u32[]{:S(2)}) %collective-permute-start.1) | collective-permute-done | bytes 64 | tf_op jit(solution)/shard_map/ppermute | solution.py:60
  193.1 10.3 %collective-permute-start.4 = (f32[2,4,256,512]{3,2,1,0:T(8,128)S(1)}, f32[2,4,256,512]{3,2,1,0:T(8,128)S(1)}, u32[]{:S(2)}, u32[]{:S(2)}) collective-permute-start(f32[2,4,256,512]{3,2,1,0:T(8,128)S(1)} %multiply_add_fusion.4), channel_id=1, source_target_pairs={{0,2},{1,3},{2,4},{3,5},{4,6},{5,7},{6,8},{7,9},{8,10},{9,11},{10,... | collective-permute-start | bytes 12582920 | tf_op jit(solution)/shard_map/ppermute | solution.py:66
  203.4 85.8 %collective-permute-done.4 = f32[2,4,256,512]{3,2,1,0:T(8,128)S(1)} collective-permute-done((f32[2,4,256,512]{3,2,1,0:T(8,128)S(1)}, f32[2,4,256,512]{3,2,1,0:T(8,128)S(1)}, u32[]{:S(2)}, u32[]{:S(2)}) %collective-permute-start.4) | collective-permute-done | bytes 4194336 | tf_op jit(solution)/shard_map/ppermute | solution.py:66
  290.3 3.9 collective-permute-start.6
  294.2 4.6 collective-permute-start.5
  298.8 84.8 %collective-permute-done.5 = f32[2,4]{1,0:T(2,128)S(1)} collective-permute-done((f32[2,4]{1,0:T(2,128)S(1)}, f32[2,4]{1,0:T(2,128)S(1)}, u32[]{:S(2)}, u32[]{:S(2)}) %collective-permute-start.5) | collective-permute-done | bytes 64 | tf_op jit(solution)/shard_map/ppermute | solution.py:65
  386.6 4.1 collective-permute-start.8
  398.2 80.7 %collective-permute-done.8 = f32[2,4,256,512]{3,2,1,0:T(8,128)S(1)} collective-permute-done((f32[2,4,256,512]{3,2,1,0:T(8,128)S(1)}, f32[2,4,256,512]{3,2,1,0:T(8,128)S(1)}, u32[]{:S(2)}, u32[]{:S(2)}) %collective-permute-start.8) | collective-permute-done | bytes 4194336 | tf_op jit(solution)/shard_map/ppermute | solution.py:66
  482.0 6.1 collective-permute-start.10
  494.5 6.1 fusion.31
  502.7 73.8 %collective-permute-done.9 = f32[2,4]{1,0:T(2,128)S(1)} collective-permute-done((f32[2,4]{1,0:T(2,128)S(1)}, f32[2,4]{1,0:T(2,128)S(1)}, u32[]{:S(2)}, u32[]{:S(2)}) %collective-permute-start.9) | collective-permute-done | bytes 64 | tf_op jit(solution)/shard_map/ppermute | solution.py:65
  576.6 6.6 multiply_add_fusion
  583.1 34.2 %bitcast_add_fusion = bf16[2,6,4,256,512]{4,1,3,2,0:T(8,128)(2,1)} fusion(f32[2,4,256,512]{3,2,1,0:T(8,128)} %multiply_add_fusion, f32[2,6,4]{1,2,0:T(4,128)S(1)} %get-tuple-element.15, bf16[2,6,4,256,512]{4,3,2,1,0:T(8,128)(2,1)} %fusion.27, f32[2,6,4]{1,2,0:T(4,128)S(1)} %reduce_window_sum.25, f32[2,6,4]{1,2,0:T(4,128)S(1)} %fusion.70, ...), kind=kOutput, calls=%fused_computation.4 | convolution fusion | flops 94372704 | bytes 29360740 | tf_op jit(solution)/shard_map/mcbh,mbhde->mchde/dot_general | solution.py:41
  617.3 18.8 %multiply_reduce_fusion = (f32[2,6,64,4]{2,3,1,0:T(4,128)S(1)}, f32[2,6,64,4,512]{4,2,3,1,0:T(8,128)}) fusion(f32[2,6,64,4]{2,3,1,0:T(4,128)S(1)} %copy-done.4, bf16[2,6,64,4,256]{4,3,2,1,0:T(4,128)(2,1)S(1)} %copy-done.2, bf16[2,6,4,256,512]{4,1,3,2,0:T(8,128)(2,1)} %bitcast_add_fusion, f32[2,6,4,512,64]{3,4,2,1,0:T(8,128)} %fusion.31), kind=kOutput, calls=%fused_computation.21 | convolution fusion | flops 813167616 | bytes 26763264 | tf_op jit(solution)/shard_map/mcihd,mchde->mcihe/dot_general | solution.py:51
  636.1 9.5 %copy.96 = f32[2,6,64,4,512]{4,3,2,1,0:T(4,128)} copy(f32[2,6,64,4,512]{4,2,3,1,0:T(8,128)} %get-tuple-element.19) | data formatting | bytes 12582912 | tf_op jit(solution)/shard_map/mul | solution.py:52
  645.6 8.5 %reshape.82 = f32[2,384,2048]{2,1,0:T(8,128)} reshape(f32[2,6,64,4,512]{4,3,2,1,0:T(4,128)} %copy.96) | data formatting | bytes 12582912 | tf_op jit(solution)/shard_map/reshape | solution.py:52
  657.9 8.5 %mul.141 = f32[2,384,2048]{2,1,0:T(8,128)} reshape(f32[2,384,4,512]{3,2,1,0:T(4,128)} %mul.140) | data formatting | bytes 12582912 | tf_op jit(solution)/shard_map/mul | solution.py:53
  666.4 14.5 %fusion.20 = bf16[2,384,2048]{2,1,0:T(8,128)(2,1)} fusion(bf16[2048,2048]{1,0:T(8,128)(2,1)} %param.13, f32[2,384,2048]{2,1,0:T(8,128)} %reshape.82, f32[2,384,2048]{2,1,0:T(8,128)} %mul.141, bf16[2,384,6144]{2,1,0:T(8,128)(2,1)} %copy-done.3, f32[2048]{0:T(1024)S(1)} %copy-done.8), kind=kOutput, calls=%fused_computation.29 | convolution fusion | flops 6458179584 | bytes 27271168 | tf_op jit(solution)/shard_map/mtc,cd->mtd/dot_general | solution.py:55
  (61 shorter events, 57.0 us)
Async XLA Ops:
  0.0 1.9 copy-start
  29.4 5.5 copy-start.3
  36.0 0.6 copy-start.5
  86.6 52.5 %copy-start.6 = (f32[2,4]{1,0:T(2,128)S(1)}, f32[2,4]{1,0:T(2,128)}, u32[]{:S(2)}) copy-start(f32[2,4]{1,0:T(2,128)} %copy-done.5) | copy-start | bytes 100
  87.3 49.9 %collective-permute-start = (f32[2,4,256,512]{3,2,1,0:T(8,128)S(1)}, f32[2,4,256,512]{3,2,1,0:T(8,128)S(1)}, u32[]{:S(2)}, u32[]{:S(2)}) collective-permute-start(f32[2,4,256,512]{3,2,1,0:T(8,128)S(1)} %bitcast.54), channel_id=1, source_target_pairs={{0,1},{1,2},{2,3},{3,4},{4,5},{5,6},{6,7},{7,8},{8,9},{9,10},{10,1... | collective-permute-start | bytes 12582920 | tf_op jit(solution)/shard_map/ppermute | solution.py:61
  137.2 54.8 %collective-permute-start.2 = (f32[2,4,256,512]{3,2,1,0:T(8,128)S(1)}, f32[2,4,256,512]{3,2,1,0:T(8,128)S(1)}, u32[]{:S(2)}, u32[]{:S(2)}) collective-permute-start(f32[2,4,256,512]{3,2,1,0:T(8,128)S(1)} %collective-permute-done), channel_id=1, source_target_pairs={{0,1},{1,2},{2,3},{3,4},{4,5},{5,6},{6,7},{7,8},{8,9},{9,10},{10,1... | collective-permute-start | bytes 12582920 | tf_op jit(solution)/shard_map/ppermute | solution.py:66
  139.1 47.9 %collective-permute-start.1 = (f32[2,4]{1,0:T(2,128)S(1)}, f32[2,4]{1,0:T(2,128)S(1)}, u32[]{:S(2)}, u32[]{:S(2)}) collective-permute-start(f32[2,4]{1,0:T(2,128)S(1)} %copy-done.6), channel_id=1, source_target_pairs={{0,1},{1,2},{2,3},{3,4},{4,5},{5,6},{6,7},{7,8},{8,9},{9,10},{10,1... | collective-permute-start | bytes 104 | tf_op jit(solution)/shard_map/ppermute | solution.py:60
  187.0 4.9 collective-permute-start.3
  193.1 96.2 %collective-permute-start.4 = (f32[2,4,256,512]{3,2,1,0:T(8,128)S(1)}, f32[2,4,256,512]{3,2,1,0:T(8,128)S(1)}, u32[]{:S(2)}, u32[]{:S(2)}) collective-permute-start(f32[2,4,256,512]{3,2,1,0:T(8,128)S(1)} %multiply_add_fusion.4), channel_id=1, source_target_pairs={{0,2},{1,3},{2,4},{3,5},{4,6},{5,7},{6,8},{7,9},{8,10},{9,11},{10,... | collective-permute-start | bytes 12582920 | tf_op jit(solution)/shard_map/ppermute | solution.py:66
  290.3 95.2 %collective-permute-start.6 = (f32[2,4,256,512]{3,2,1,0:T(8,128)S(1)}, f32[2,4,256,512]{3,2,1,0:T(8,128)S(1)}, u32[]{:S(2)}, u32[]{:S(2)}) collective-permute-start(f32[2,4,256,512]{3,2,1,0:T(8,128)S(1)} %multiply_add_fusion.3), channel_id=1, source_target_pairs={{0,4},{1,5},{2,6},{3,7},{4,8},{5,9},{6,10},{7,11},{8,12},{9,13},{1... | collective-permute-start | bytes 12582920 | tf_op jit(solution)/shard_map/ppermute | solution.py:66
  294.2 89.4 %collective-permute-start.5 = (f32[2,4]{1,0:T(2,128)S(1)}, f32[2,4]{1,0:T(2,128)S(1)}, u32[]{:S(2)}, u32[]{:S(2)}) collective-permute-start(f32[2,4]{1,0:T(2,128)S(1)} %get-tuple-element.10), channel_id=1, source_target_pairs={{0,2},{1,3},{2,4},{3,5},{4,6},{5,7},{6,8},{7,9},{8,10},{9,11},{10,... | collective-permute-start | bytes 104 | tf_op jit(solution)/shard_map/ppermute | solution.py:65
  386.6 92.4 %collective-permute-start.8 = (f32[2,4,256,512]{3,2,1,0:T(8,128)S(1)}, f32[2,4,256,512]{3,2,1,0:T(8,128)S(1)}, u32[]{:S(2)}, u32[]{:S(2)}) collective-permute-start(f32[2,4,256,512]{3,2,1,0:T(8,128)S(1)} %multiply_add_fusion.2), channel_id=1, source_target_pairs={{0,8},{1,9},{2,10},{3,11},{4,12},{5,13},{6,14},{7,15},{8,16},{9,17... | collective-permute-start | bytes 12582920 | tf_op jit(solution)/shard_map/ppermute | solution.py:66
  390.6 7.0 %collective-permute-start.7 = (f32[2,4]{1,0:T(2,128)S(1)}, f32[2,4]{1,0:T(2,128)S(1)}, u32[]{:S(2)}, u32[]{:S(2)}) collective-permute-start(f32[2,4]{1,0:T(2,128)S(1)} %get-tuple-element.8), channel_id=1, source_target_pairs={{0,4},{1,5},{2,6},{3,7},{4,8},{5,9},{6,10},{7,11},{8,12},{9,13},{1... | collective-permute-start | bytes 104 | tf_op jit(solution)/shard_map/ppermute | solution.py:65
  482.0 94.6 %collective-permute-start.10 = (f32[2,4,256,512]{3,2,1,0:T(8,128)}, f32[2,4,256,512]{3,2,1,0:T(8,128)}, u32[]{:S(2)}, u32[]{:S(2)}) collective-permute-start(f32[2,4,256,512]{3,2,1,0:T(8,128)} %multiply_add_fusion.1), channel_id=1, source_target_pairs={{0,16},{1,17},{2,18},{3,19},{4,20},{5,21},{6,22},{7,23},{8,24},{9,... | collective-permute-start | bytes 12582920 | tf_op jit(solution)/shard_map/ppermute | solution.py:66
  494.5 6.1 copy-start.7
  500.6 75.9 %collective-permute-start.9 = (f32[2,4]{1,0:T(2,128)S(1)}, f32[2,4]{1,0:T(2,128)S(1)}, u32[]{:S(2)}, u32[]{:S(2)}) collective-permute-start(f32[2,4]{1,0:T(2,128)S(1)} %copy-done.7), channel_id=1, source_target_pairs={{0,8},{1,9},{2,10},{3,11},{4,12},{5,13},{6,14},{7,15},{8,16},{9,17... | collective-permute-start | bytes 104 | tf_op jit(solution)/shard_map/ppermute | solution.py:65
  583.1 34.2 %copy-start.2 = (bf16[2,6,64,4,256]{4,3,2,1,0:T(4,128)(2,1)S(1)}, bf16[2,6,64,4,256]{4,3,2,1,0:T(4,128)(2,1)}, u32[]{:S(2)}) copy-start(bf16[2,6,64,4,256]{4,3,2,1,0:T(4,128)(2,1)} %reshape.79) | copy-start | bytes 4718596
  583.1 34.2 %copy-start.4 = (f32[2,6,64,4]{2,3,1,0:T(4,128)S(1)}, f32[2,6,64,4]{2,3,1,0:T(4,128)}, u32[]{:S(2)}) copy-start(f32[2,6,64,4]{2,3,1,0:T(4,128)} %copy.95) | copy-start | bytes 36868
  657.9 8.5 %copy-start.8 = (f32[2048]{0:T(1024)S(1)}, f32[2048]{0:T(1024)}, u32[]{:S(2)}) copy-start(f32[2048]{0:T(1024)} %param.12) | copy-start | bytes 24580
  666.4 14.5 %copy-start.1 = (bf16[2,384,2048]{2,1,0:T(8,128)(2,1)S(1)}, bf16[2,384,2048]{2,1,0:T(8,128)(2,1)}, u32[]{:S(2)}) copy-start(bf16[2,384,2048]{2,1,0:T(8,128)(2,1)} %param.7) | copy-start | bytes 9437188
where the time goes:
time: 690 us; the launch traced here: 681 us
  waiting for transfers between devices  422 us (61%)
  matrix products  138 us (20%)
  local copies, waits for them, and re-layouts  56.2 us (8%)
  starting transfers between devices  47.4 us (7%)
  other arithmetic  17.2 us (2%)
    ppermute x5, waiting for transfers between devices, incoming_state(): prev_state = lax.ppermute(acc_state, 'sp', send_pairs)  168 us
    ppermute x4, waiting for transfers between devices, incoming_state(): prev_decay = lax.ppermute(acc_decay, 'sp', send_pairs)  164 us
    ppermute x1, waiting for transfers between devices, incoming_state(): acc_state = lax.ppermute(local_state, 'sp', shift_pairs)  47.9 us
    ppermute x1, waiting for transfers between devices, incoming_state(): acc_decay = lax.ppermute(shard_tot, 'sp', shift_pairs)  42.1 us
    dot_general x1, matrix products, local_parts(): start_state = jnp.einsum('mcbh,mbhde->mchde', pass_weight, chunk_state)  34.2 us
    dot_general x1, matrix products, local_parts(): jnp.einsum('mbh,mbhde->mhde', jnp.exp(shard_tot[:, None, :] - chunk_end),...  27.1 us
    ppermute x5, starting transfers between devices, incoming_state(): prev_state = lax.ppermute(acc_state, 'sp', send_pairs)  26.3 us
    dot_general x1, matrix products, local_parts(): jnp.einsum('mtd,dc->mtc', x_loc, w_in, preferred_element_type=jnp.float32)  22.9 us
  transfers between devices with their start and end apart: 11, of which 9 were waited for; matrix products, arithmetic and copies ran while one was open for 2% of the time, Pallas kernels for 0%

commit v1 on v0

v1 whole, which is shorter than its diff:
```python
import functools

import jax
import jax.numpy as jnp
from jax import lax
from jax.experimental import pallas as pl
from jax.experimental.pallas import tpu as pltpu
from jax.sharding import PartitionSpec as P

NORM_EPS = 1e-6
CORES = 2
PIECES = 16
LAG = 4
MESH = pl.DeviceIdType.MESH
F32 = jnp.float32
BF16 = jnp.bfloat16


def chip_grid(chips):
    nx = int(chips ** 0.5)
    while chips % nx:
        nx -= 1
    return chips // nx, nx


def layer_kernel(ny, nx, hidden, w_in, w_gate, gate_bias, a_log, norm_w, w_out, out,
                 x_v, w_v, wo_v, wg_v, par_v, proj, intra, acc, y_v,
                 cl, clt, etail, ecum, dtile, dbuf, coef,
                 state, c_in, f_in, g_in, c_out, f_out, g_out,
                 x_sem, xs_sem, xr_sem, w_sem, wo_sem, ds_sem, dr_sem, send_sem, recv_sem, o_sem, os_sem, or_sem):
    rows = hidden.shape[1]
    n_heads = w_gate.shape[1]
    val_dim = w_out.shape[0]
    key_dim = (w_in.shape[1] - 2 * val_dim) // 2
    head_k, head_v = key_dim // n_heads, val_dim // n_heads
    blk = head_k + head_v
    tiles = blk // head_k
    total = n_heads * PIECES
    prow = head_k // 8 // PIECES
    hrow = head_k // 8

    me = lax.axis_index('sp')
    core = lax.rem(me, CORES)
    chip = lax.div(me, CORES)
    x = lax.rem(chip, nx)
    y = lax.div(chip, nx)

    def device(yy, xx, cc):
        return {'sp': (yy * nx + xx) * CORES + cc}

    partner = device(y, x, 1 - core)
    down = device(lax.rem(y + 1, ny), x, core)
    up = device(lax.rem(y + ny - 1, ny), x, core)
    right = device(y, lax.rem(x + 1, nx), core)
    left = device(y, lax.rem(x + nx - 1, nx), core)

    def mate(offset):
        return device(y, lax.rem(x + offset, nx), core)

    x_load = pltpu.make_async_copy(hidden.at[core], x_v.at[core], x_sem)
    x_load.start()

    def w_copies(seq, is_kv, h):
        slot = lax.rem(seq, 3)
        k_at = jnp.where(is_kv, key_dim, 0) + h * head_k
        v_at = 2 * key_dim + jnp.where(is_kv, 0, val_dim) + h * head_v
        return (
            pltpu.make_async_copy(w_in.at[:, pl.ds(pl.multiple_of(k_at, 128), head_k)], w_v.at[slot, :, 0:head_k], w_sem.at[slot, 0]),
            pltpu.make_async_copy(w_in.at[:, pl.ds(pl.multiple_of(v_at, 128), head_v)], w_v.at[slot, :, head_k:blk], w_sem.at[slot, 1]),
        )

    def w_start(seq, is_kv, h):
        for copy in w_copies(seq, is_kv, h):
            copy.start()

    def w_wait(seq, is_kv, h):
        for copy in w_copies(seq, is_kv, h):
            copy.wait()

    def wo_copy(h):
        slot = lax.rem(h, 2)
        return pltpu.make_async_copy(w_out.at[pl.ds(pl.multiple_of(h * head_v, 128), head_v), :], wo_v.at[slot], wo_sem.at[slot])

    w_start(0, True, 0)

    barrier = pltpu.get_barrier_semaphore()
    peers = [partner, down, up] + [mate(o) for o in range(1, nx)]
    for peer in peers:
        pl.semaphore_signal(barrier, inc=1, device_id=peer, device_id_type=MESH)
    pl.semaphore_wait(barrier, len(peers))

    x_send = pltpu.make_async_remote_copy(hidden.at[1 - core], x_v.at[core], xs_sem, xr_sem, device_id=partner, device_id_type=MESH)
    x_send.start()
    x_recv = pltpu.make_async_remote_copy(hidden.at[1 - core], x_v.at[1 - core], xs_sem, xr_sem, device_id=partner, device_id_type=MESH)
    w_start(1, True, 1)
    w_start(2, False, 0)

    wg_v[...] = jnp.zeros_like(wg_v)
    wg_v[:, 0:n_heads] = w_gate[...]
    par_v[...] = jnp.zeros_like(par_v)
    par_v[0:1, 0:n_heads] = gate_bias[...]
    par_v[8:9, 0:n_heads] = a_log[...]

    @pl.when(y == 0)
    def _():
        c_in[...] = jnp.zeros_like(c_in)
        g_in[...] = jnp.zeros_like(g_in)

    @pl.when(jnp.logical_and(y > 0, x == nx - 1))
    def _():
        g_in[...] = jnp.zeros_like(g_in)

    @pl.when(x == 0)
    def _():
        f_in[...] = jnp.zeros_like(f_in)

    lane = lax.broadcasted_iota(jnp.int32, (1, 128), 1)

    def gate_half(b):
        logit = jnp.dot(x_v[b], wg_v[...], preferred_element_type=F32) + par_v[0:1, :]
        soft = jnp.maximum(logit, 0.0) + jnp.log1p(jnp.exp(-jnp.abs(logit)))
        decay = -jnp.exp(par_v[8:9, :]) * soft
        tri = lax.broadcasted_iota(jnp.int32, (rows, rows), 0) >= lax.broadcasted_iota(jnp.int32, (rows, rows), 1)
        cum = jnp.dot(jnp.where(tri, 1.0, 0.0).astype(F32), decay, precision=lax.Precision.HIGHEST, preferred_element_type=F32)
        cl[b] = cum
        clt[b] = jnp.transpose(cum)

    def proj_half(b):
        def one(j, carry):
            cols = pl.ds(pl.multiple_of(j * head_k, 128), head_k)
            part = jnp.dot(x_v[b], w_v[0, :, cols], preferred_element_type=F32)
            proj[0, b, :, cols] = part.astype(BF16)
            return carry
        lax.fori_loop(0, tiles, one, 0)

    x_load.wait()
    gate_half(core)
    w_wait(0, True, 0)
    proj_half(core)
    x_recv.wait_recv()
    gate_half(1 - core)

    tot0 = cl[0, rows - 1:rows, :]
    tot1 = cl[1, rows - 1:rows, :]
    own = jnp.broadcast_to(tot0 + tot1, (8, 128))
    dtile[...] = own
    dbuf[x] = own

    def d_copy(offset, source):
        return pltpu.make_async_remote_copy(dtile, dbuf.at[source], ds_sem.at[offset - 1], dr_sem.at[offset - 1], device_id=mate(offset), device_id_type=MESH)

    for o in range(1, nx):
        d_copy(o, x).start()
    etail[0] = jnp.exp((tot0 - cl[0]) + tot1)
    etail[1] = jnp.exp(tot1 - cl[1])
    ecum[0] = jnp.exp(cl[0])
    ecum[1] = jnp.exp(cl[1] + tot0)
    proj_half(1 - core)
    w_start(3, True, 2)
    wo_copy(0).start()
    wo_copy(1).start()

    def column(ref, b, h):
        return jnp.sum(jnp.where(lane == h, ref[b], 0.0), axis=1, keepdims=True)

    def row_of(b, h):
        sub = lax.broadcasted_iota(jnp.int32, (8, 1), 0)
        return jnp.sum(jnp.where(sub == h, clt[b, 0:8, :], 0.0), axis=0, keepdims=True)

    def chip_state(h):
        out_sum = None
        for b in range(2):
            keys = proj[h, b, :, 0:head_k].astype(F32) * column(etail, b, h)
            vals = proj[h, b, :, head_k:blk].astype(F32)
            part = lax.dot_general(keys, vals, (((0,), (0,)), ((), ())), preferred_element_type=F32)
            out_sum = part if out_sum is None else out_sum + part
        state[pl.ds(h * hrow, hrow)] = out_sum.reshape(hrow, 8, head_v)

    chip_state(0)
    for o in range(1, nx):
        d_copy(o, lax.rem(x + nx - o, nx)).wait_recv()
    logs = [dbuf[i] for i in range(nx)]
    zero = jnp.zeros((8, 128), F32)
    log_row, log_start, log_end = zero, zero, zero
    for i in range(nx):
        log_row = log_row + logs[i]
        log_start = log_start + jnp.where(i < x, logs[i], 0.0)
        log_end = log_end + jnp.where(i > x, logs[i], 0.0)
    for kind, log_w in enumerate((own, log_start, log_end, log_row)):
        for h in range(n_heads):
            one = jnp.sum(jnp.where(lane == h, log_w, 0.0), axis=1, keepdims=True)
            coef[kind, h] = jnp.broadcast_to(jnp.exp(one), (8, head_v))

    def piece(ref, p):
        return ref.at[pl.ds(p * prow, prow)]

    def flow(kind, src, dst, p, target):
        return pltpu.make_async_remote_copy(piece(src, p), piece(dst, p), send_sem.at[kind, p], recv_sem.at[kind, p], device_id=target, device_id_type=MESH)

    c_sends, c_recvs = y < ny - 1, y > 0
    f_sends, f_recvs = x < nx - 1, x > 0
    g_sends, g_recvs = jnp.logical_and(y > 0, x > 0), jnp.logical_and(y > 0, x < nx - 1)

    def comm(s):
        def at(lag):
            p = s - lag * LAG
            return p, jnp.logical_and(p >= 0, p < total)

        p, live = at(y)

        @pl.when(jnp.logical_and(live, c_recvs))
        def _(p=p):
            flow(0, c_out, c_in, p, down).wait_recv()

        @pl.when(jnp.logical_and(live, c_sends))
        def _(p=p):
            h = lax.div(p, PIECES)
            at_p = pl.ds(p * prow, prow)
            c_out[at_p] = coef[3, h] * c_in[at_p] + coef[2, h] * state[at_p]
            flow(0, c_out, c_in, p, down).start()

        p, live = at(y + x)

        @pl.when(jnp.logical_and(live, f_recvs))
        def _(p=p):
            flow(1, f_out, f_in, p, right).wait_recv()

        @pl.when(jnp.logical_and(live, f_sends))
        def _(p=p):
            h = lax.div(p, PIECES)
            at_p = pl.ds(p * prow, prow)
            f_out[at_p] = coef[0, h] * (f_in[at_p] + coef[1, h] * c_in[at_p]) + state[at_p]
            flow(1, f_out, f_in, p, right).start()

        p, live = at(y + nx - 1 - x)

        @pl.when(jnp.logical_and(live, g_recvs))
        def _(p=p):
            flow(2, g_out, g_in, p, left).wait_recv()

        @pl.when(jnp.logical_and(live, g_sends))
        def _(p=p):
            at_p = pl.ds(p * prow, prow)
            g_out[at_p] = g_in[at_p] + c_in[at_p]
            flow(2, g_out, g_in, p, left).start()

        p, live = at(y + jnp.maximum(x, nx - 1 - x))

        @pl.when(live)
        def _(p=p):
            h = lax.div(p, PIECES)
            at_p = pl.ds(p * prow, prow)
            state[at_p] = f_in[at_p] + coef[1, h] * (c_in[at_p] + g_in[at_p])

    def comm_steps(s, n):
        lax.fori_loop(0, n, lambda i, c: (comm(s + i), c)[1], 0)

    def proj_tile(seq, dest, j):
        slot = lax.rem(seq, 3)
        cols = pl.ds(pl.multiple_of(j * head_k, 128), head_k)
        rows_all = x_v[...].reshape(2 * rows, x_v.shape[2])
        part = jnp.dot(rows_all, w_v[slot, :, cols], preferred_element_type=F32)
        proj[dest, :, :, cols] = part.astype(BF16).reshape(2, rows, head_k)

    def intra_block(h, b):
        q = proj[n_heads + h, b, :, 0:head_k]
        cum_i = column(cl, b, h)
        causal = lax.broadcasted_iota(jnp.int32, (rows, rows), 0) >= lax.broadcasted_iota(jnp.int32, (rows, rows), 1)
        o = None
        for src in range(b + 1):
            keys = proj[h, src, :, 0:head_k]
            vals = proj[h, src, :, head_k:blk].astype(F32)
            score = lax.dot_general(q, keys, (((1,), (1,)), ((), ())), preferred_element_type=F32)
            cum_j = row_of(src, h)
            if src == b:
                weight = jnp.where(causal, jnp.exp(jnp.where(causal, cum_i - cum_j, 0.0)), 0.0)
            else:
                weight = jnp.exp(cum_i + (cum_j[:, rows - 1:rows] - cum_j))
            part = jnp.dot(score * weight, vals, preferred_element_type=F32)
            o = part if o is None else o + part
        intra[h, b] = o

    half_rows = rows // 6
    scale = head_k ** -0.5

    def finish_half(h, b, last):
        q = proj[n_heads + h, b, :, 0:head_k].astype(F32)
        entering = state[pl.ds(h * hrow, hrow)].reshape(head_k, head_v)
        inter = jnp.dot(q, entering, preferred_element_type=F32) * column(ecum, b, h)
        intra[h, b] = (intra[h, b] + inter) * scale
        gain = norm_w[0:1, pl.ds(pl.multiple_of(h * head_v, 128), head_v)]

        def norm(i, carry):
            at_r = pl.ds(pl.multiple_of(i * half_rows, 16), half_rows)
            o = intra[h, b, at_r, :]
            z = proj[n_heads + h, b, at_r, head_k:blk].astype(F32)
            n = o * lax.rsqrt(jnp.mean(o * o, axis=1, keepdims=True) + NORM_EPS) * gain
            y_v[at_r, :] = (n * (z / (1.0 + jnp.exp(-z)))).astype(BF16)
            return carry
        lax.fori_loop(0, rows // half_rows, norm, 0)

        def project(j, carry):
            cols = pl.ds(pl.multiple_of(j * head_v, 128), head_v)
            part = jnp.dot(y_v[...], wo_v[lax.rem(h, 2), :, cols], preferred_element_type=F32)
            if last:
                x_v[b, :, cols] = (acc[b, :, cols] + part).astype(BF16)
            else:
                acc[b, :, cols] = acc[b, :, cols] + part
            return carry
        lax.fori_loop(0, w_out.shape[1] // head_v, project, 0)

    per = PIECES // 8

    def round_body(h, carry):
        s0 = (h - 1) * PIECES
        w_wait(2 * h - 1, True, h)

        def kv_tile(j, c):
            proj_tile(2 * h - 1, h, j)
            comm_steps(s0 + j * per, per)
            return c
        lax.fori_loop(0, tiles, kv_tile, 0)
        w_start(2 * h + 2, False, h)
        chip_state(h)
        comm_steps(s0 + 3 * per, per)
        w_wait(2 * h, False, h - 1)

        def qz_tile(j, c):
            proj_tile(2 * h, n_heads + h - 1, j)
            comm_steps(s0 + (4 + j) * per, per)
            return c
        lax.fori_loop(0, tiles, qz_tile, 0)

        @pl.when(h == 1)
        def _():
            w_start(2 * h + 3, True, h + 2)
        intra_block(h - 1, 0)
        comm_steps(s0 + 7 * per, per)
        intra_block(h - 1, 1)
        return carry
    lax.fori_loop(1, n_heads, round_body, 0)

    last_head = n_heads - 1
    lags = (ny - 1 + nx - 1) * LAG
    s1 = last_head * PIECES
    w_wait(2 * n_heads, False, last_head)
    acc[...] = jnp.zeros_like(acc)
    each = lags // 8

    def last_tile(j, c):
        proj_tile(2 * n_heads, n_heads + last_head, j)
        comm_steps(s1 + j * each, each)
        return c
    lax.fori_loop(0, tiles, last_tile, 0)
    intra_block(last_head, 0)
    comm_steps(s1 + 3 * each, each)
    intra_block(last_head, 1)

    def early(i, c):
        h = lax.div(i, 2)

        @pl.when(lax.rem(i, 2) == 0)
        def _():
            wo_copy(h).wait()
        finish_half(h, lax.rem(i, 2), False)

        @pl.when(jnp.logical_and(lax.rem(i, 2) == 1, h + 2 < n_heads))
        def _():
            wo_copy(h + 2).start()
        n = jnp.where(i < 3, each, jnp.where(i == 3, lags - 7 * each, 2))
        at_s = s1 + jnp.where(i < 4, (4 + i) * each, lags + (i - 4) * 2)
        lax.fori_loop(0, n, lambda k, cc: (comm(at_s + k), cc)[1], 0)
        return c
    lax.fori_loop(0, 2 * last_head, early, 0)
    done = lags + (2 * last_head - 4) * 2
    comm_steps(s1 + done, total + lags - s1 - done)

    wo_copy(last_head).wait()
    finish_half(last_head, 1 - core, True)
    o_send = pltpu.make_async_remote_copy(x_v.at[1 - core], out.at[core], os_sem, or_sem, device_id=partner, device_id_type=MESH)
    o_send.start()
    finish_half(last_head, core, True)
    o_store = pltpu.make_async_copy(x_v.at[core], out.at[core], o_sem)
    o_store.start()

    x_send.wait_send()
    for o in range(1, nx):
        d_copy(o, x).wait_send()

    def drain(p, c):
        @pl.when(c_sends)
        def _():
            flow(0, c_out, c_in, p, down).wait_send()

        @pl.when(f_sends)
        def _():
            flow(1, f_out, f_in, p, right).wait_send()

        @pl.when(g_sends)
        def _():
            flow(2, g_out, g_in, p, left).wait_send()
        return c
    lax.fori_loop(0, total, drain, 0)
    o_store.wait()
    o_send.wait_send()
    pltpu.make_async_remote_copy(x_v.at[1 - core], out.at[1 - core], os_sem, or_sem, device_id=partner, device_id_type=MESH).wait_recv()


def solution(mesh):
    ny, nx = chip_grid(mesh.shape['sp'] // CORES)

    def device_body(hidden, w_in, w_gate, gate_bias, a_log, norm_w, w_out):
        _, rows, d_model = hidden.shape
        n_heads = w_gate.shape[1]
        val_dim = w_out.shape[0]
        key_dim = (w_in.shape[1] - 2 * val_dim) // 2
        head_k, head_v = key_dim // n_heads, val_dim // n_heads
        blk = head_k + head_v
        total = n_heads * PIECES
        any_space = pl.BlockSpec(memory_space=pl.ANY)
        vmem = pl.BlockSpec(memory_space=pltpu.VMEM)
        flow_buf = pltpu.VMEM((n_heads * head_k // 8, 8, head_v), F32)
        dma = pltpu.SemaphoreType.DMA
        return pl.pallas_call(
            functools.partial(layer_kernel, ny, nx),
            out_shape=jax.ShapeDtypeStruct(hidden.shape, BF16),
            in_specs=[any_space, any_space, vmem, vmem, vmem, vmem, any_space],
            out_specs=any_space,
            scratch_shapes=[
                pltpu.VMEM((2, rows, d_model), BF16),
                pltpu.VMEM((3, d_model, blk), BF16),
                pltpu.VMEM((2, head_v, w_out.shape[1]), BF16),
                pltpu.VMEM((d_model, 128), BF16),
                pltpu.VMEM((16, 128), F32),
                pltpu.VMEM((2 * n_heads, 2, rows, blk), BF16),
                pltpu.VMEM((n_heads, 2, rows, head_v), F32),
                pltpu.VMEM((2, rows, w_out.shape[1]), F32),
                pltpu.VMEM((rows, head_v), BF16),
                pltpu.VMEM((2, rows, 128), F32),
                pltpu.VMEM((2, 128, rows), F32),
                pltpu.VMEM((2, rows, 128), F32),
                pltpu.VMEM((2, rows, 128), F32),
                pltpu.VMEM((8, 128), F32),
                pltpu.VMEM((nx, 8, 128), F32),
                pltpu.VMEM((4, n_heads, 8, head_v), F32),
                flow_buf, flow_buf, flow_buf, flow_buf, flow_buf, flow_buf, flow_buf,
                dma, dma, dma, dma((3, 2)), dma((2,)), dma((nx - 1,)), dma((nx - 1,)),
                dma((3, total)), dma((3, total)), dma, dma, dma,
            ],
            compiler_params=pltpu.CompilerParams(collective_id=0, has_side_effects=True, vmem_limit_bytes=67043328),
        )(hidden, w_in, w_gate, gate_bias.reshape(1, -1), a_log.reshape(1, -1), norm_w.reshape(1, -1), w_out)

    return jax.shard_map(device_body, mesh=mesh, in_specs=(P('dp', 'sp', None), P(), P(), P(), P(), P(), P()), out_specs=P('dp', 'sp', None), check_vma=False)
```

time: 690 us -> 108 us (0.16)
  the two profiles are of different devices: /device:TPU:110 before, /device:TPU:120 now
where the time goes in v1:
time: 108 us
  Pallas kernels  102 us (94%)
  local copies, waits for them, and re-layouts  5.74 us (5%)
    pallas_call x1, Pallas kernels, device_body(): pl.pallas_call(functools.partial(layer_kernel, ny, nx), out_shape=jax.Sha...  102 us
    unnamed x2, local copies, waits for them, and re-layouts  5.74 us

profile of v1, /device:TPU:120, one launch (start us, length us, event | category | flops | bytes accessed | tf_op | source)
XLA Modules:
  0.0 108.2 jit_solution(10924293563626161920)
XLA Ops:
  0.0 1.8 %copy.8.w_gate = bf16[2048,4]{1,0:T(8,128)(2,1)} copy(bf16[2048,4]{0,1:T(4,128)(2,1)} %param.9) | data formatting | bytes 32768 | tf_op args[2]
  1.8 102.4 %shard_map.73 = bf16[2,384,2048]{2,1,0:T(8,128)(2,1)} custom-call(bf16[2,384,2048]{2,1,0:T(8,128)(2,1)} %hidden.1, bf16[2048,6144]{1,0:T(8,128)(2,1)} %w_in.1, bf16[2048,4]{1,0:T(8,128)(2,1)} %copy.8.w_gate, f32[1,4]{1,0:T(1,128)} %bitcast.4, f32[1,4]{1,0:T(1,128)} %bitcast.5, f32[1,2048]{1,0:T(1,128)} %bitcast.3, bf16[2048,2048]{1,0:T(8,128)(2,1)} %w_out.1), custom_call_target="tpu_custom_call" | custom-call | tf_op jit(solution)/shard_map/pallas_call | solution.py:424
  104.2 4.0 %copy.10 = bf16[2,384,2048]{2,1,0:T(8,128)(2,1)} copy(bf16[2,384,2048]{2,1,0:T(8,128)(2,1)} %shard_map.73) | data formatting | bytes 6291456

commit v2 on v1

v2 whole, which is shorter than its diff:
```python
import functools

import jax
import jax.numpy as jnp
from jax import lax
from jax.experimental import pallas as pl
from jax.experimental.pallas import tpu as pltpu
from jax.sharding import PartitionSpec as P

NORM_EPS = 1e-6
CORES = 2
PIECES = 8
LAG = 3
MESH = pl.DeviceIdType.MESH
F32 = jnp.float32
BF16 = jnp.bfloat16


def chip_grid(chips):
    nx = int(chips ** 0.5)
    while chips % nx:
        nx -= 1
    return chips // nx, nx


def layer_kernel(ny, nx, hidden, w_in, w_gate, gate_bias, a_log, norm_w, w_out, out,
                 x_v, w_v, wo_v, wg_v, par_v, proj, intra, acc, y_v,
                 cl, clt, etail, ecum, dtile, dbuf, coef,
                 state, c_in, f_in, g_in, c_out, f_out, g_out,
                 x_sem, xs_sem, xr_sem, w_sem, wo_sem, ds_sem, dr_sem, send_sem, recv_sem, o_sem, os_sem, or_sem):
    rows = hidden.shape[1]
    n_heads = w_gate.shape[0]
    val_dim = w_out.shape[0]
    key_dim = (w_in.shape[1] - 2 * val_dim) // 2
    head_k, head_v = key_dim // n_heads, val_dim // n_heads
    blk = head_k + head_v
    tiles = blk // head_k
    total = n_heads * PIECES
    prow = head_k // 8 // PIECES
    hrow = head_k // 8

    me = lax.axis_index('sp')
    core = lax.rem(me, CORES)
    chip = lax.div(me, CORES)
    x = lax.rem(chip, nx)
    y = lax.div(chip, nx)

    def device(yy, xx, cc):
        return {'sp': (yy * nx + xx) * CORES + cc}

    partner = device(y, x, 1 - core)
    down = device(lax.rem(y + 1, ny), x, core)
    up = device(lax.rem(y + ny - 1, ny), x, core)
    right = device(y, lax.rem(x + 1, nx), core)
    left = device(y, lax.rem(x + nx - 1, nx), core)

    def mate(offset):
        return device(y, lax.rem(x + offset, nx), core)

    x_load = pltpu.make_async_copy(hidden.at[core], x_v.at[core], x_sem)
    x_load.start()

    def w_copies(seq, is_kv, h):
        slot = lax.rem(seq, 3)
        k_at = jnp.where(is_kv, key_dim, 0) + h * head_k
        v_at = 2 * key_dim + jnp.where(is_kv, 0, val_dim) + h * head_v
        return (
            pltpu.make_async_copy(w_in.at[:, pl.ds(pl.multiple_of(k_at, 128), head_k)], w_v.at[slot, :, 0:head_k], w_sem.at[slot, 0]),
            pltpu.make_async_copy(w_in.at[:, pl.ds(pl.multiple_of(v_at, 128), head_v)], w_v.at[slot, :, head_k:blk], w_sem.at[slot, 1]),
        )

    def kv_seq(h):
        return jnp.maximum(2 * h - 1, 0)

    def qz_seq(h):
        return 2 * h + 2

    def w_start(seq, is_kv, h):
        for copy in w_copies(seq, is_kv, h):
            copy.start()

    def w_wait(seq, is_kv, h):
        for copy in w_copies(seq, is_kv, h):
            copy.wait()

    def wo_copy(h):
        slot = lax.rem(h, 2)
        return pltpu.make_async_copy(w_out.at[pl.ds(pl.multiple_of(h * head_v, 128), head_v), :], wo_v.at[slot], wo_sem.at[slot])

    w_start(kv_seq(0), True, 0)

    barrier = pltpu.get_barrier_semaphore()
    peers = [partner, down, up] + [mate(o) for o in range(1, nx)]
    for peer in peers:
        pl.semaphore_signal(barrier, inc=1, device_id=peer, device_id_type=MESH)
    wg_v[...] = jnp.zeros_like(wg_v)
    wg_v[0:n_heads, :] = w_gate[...]
    par_v[...] = jnp.zeros_like(par_v)
    par_v[0:1, 0:n_heads] = gate_bias[...]
    par_v[8:9, 0:n_heads] = a_log[...]
    pl.semaphore_wait(barrier, len(peers))

    x_send = pltpu.make_async_remote_copy(hidden.at[1 - core], x_v.at[core], xs_sem, xr_sem, device_id=partner, device_id_type=MESH)
    x_send.start()
    x_recv = pltpu.make_async_remote_copy(hidden.at[1 - core], x_v.at[1 - core], xs_sem, xr_sem, device_id=partner, device_id_type=MESH)
    w_start(kv_seq(1), True, 1)
    w_start(qz_seq(0), False, 0)

    lane = lax.broadcasted_iota(jnp.int32, (1, 128), 1)
    tri = (lax.broadcasted_iota(jnp.int32, (128, 128), 0) >= lax.broadcasted_iota(jnp.int32, (128, 128), 1))

    def gate_half(b):
        logit = lax.dot_general(x_v[b], wg_v[...], (((1,), (1,)), ((), ())), preferred_element_type=F32) + par_v[0:1, :]
        soft = jnp.maximum(logit, 0.0) + jnp.log1p(jnp.exp(-jnp.abs(logit)))
        cl[b] = -jnp.exp(par_v[8:9, :]) * soft
        ones = jnp.where(tri, 1.0, 0.0).astype(BF16)

        def run(i, before):
            at_r = pl.ds(pl.multiple_of(i * 128, 128), 128)
            decay = cl[b, at_r, :]
            top = decay.astype(BF16)
            rest = decay - top.astype(F32)
            mid = rest.astype(BF16)
            low = (rest - mid.astype(F32)).astype(BF16)
            sums = jnp.dot(ones, jnp.concatenate([top, mid, low], axis=1), preferred_element_type=F32)
            cum = before + (sums[:, 0:128] + (sums[:, 128:256] + sums[:, 256:384]))
            cl[b, at_r, :] = cum
            clt[b, :, at_r] = jnp.transpose(cum)
            return cum[127:128, :]
        lax.fori_loop(0, rows // 128, run, jnp.zeros((1, 128), F32))

    def proj_half(seq, dest, j, b):
        cols = pl.ds(pl.multiple_of(j * head_k, 128), head_k)
        part = jnp.dot(x_v[b], w_v[lax.rem(seq, 3), :, cols], preferred_element_type=F32)
        proj[dest, b, :, cols] = part.astype(BF16)

    def d_copy(offset, source):
        return pltpu.make_async_remote_copy(dtile, dbuf.at[source], ds_sem.at[offset - 1], dr_sem.at[offset - 1], device_id=mate(offset), device_id_type=MESH)

    def chip_decays():
        tot0 = cl[0, rows - 1:rows, :]
        tot1 = cl[1, rows - 1:rows, :]
        own = jnp.broadcast_to(tot0 + tot1, (8, 128))
        dtile[...] = own
        dbuf[x] = own
        for o in range(1, nx):
            d_copy(o, x).start()

        def powers(i, carry):
            at_r = pl.ds(pl.multiple_of(i * 64, 64), 64)
            etail[0, at_r, :] = jnp.exp((tot0 - cl[0, at_r, :]) + tot1)
            etail[1, at_r, :] = jnp.exp(tot1 - cl[1, at_r, :])
            ecum[0, at_r, :] = jnp.exp(cl[0, at_r, :])
            ecum[1, at_r, :] = jnp.exp(cl[1, at_r, :] + tot0)
            return carry
        lax.fori_loop(0, rows // 64, powers, 0)

    def column(ref, b, h):
        return jnp.sum(jnp.where(lane == h, ref[b], 0.0), axis=1, keepdims=True)

    def row_of(b, h):
        sub = lax.broadcasted_iota(jnp.int32, (8, 1), 0)
        return jnp.sum(jnp.where(sub == h, clt[b, 0:8, :], 0.0), axis=0, keepdims=True)

    def chip_state(h):
        out_sum = None
        for b in range(2):
            keys = proj[h, b, :, 0:head_k].astype(F32) * column(etail, b, h)
            vals = proj[h, b, :, head_k:blk].astype(F32)
            part = lax.dot_general(keys, vals, (((0,), (0,)), ((), ())), preferred_element_type=F32)
            out_sum = part if out_sum is None else out_sum + part
        state[pl.ds(h * hrow, hrow)] = out_sum.reshape(hrow, 8, head_v)

    def row_weights():
        for o in range(1, nx):
            d_copy(o, lax.rem(x + nx - o, nx)).wait_recv()
        zero = jnp.zeros((8, 128), F32)
        log_row, log_start, log_end = zero, zero, zero
        for i in range(nx):
            log_i = dbuf[i]
            log_row = log_row + log_i
            log_start = log_start + jnp.where(i < x, log_i, 0.0)
            log_end = log_end + jnp.where(i > x, log_i, 0.0)
        for kind, log_w in enumerate((dtile[...], log_start, log_end, log_row)):
            for h in range(n_heads):
                one = jnp.sum(jnp.where(lane == h, log_w, 0.0), axis=1, keepdims=True)
                coef[kind, h] = jnp.broadcast_to(jnp.exp(one), (8, head_v))

    def piece(ref, p):
        return ref.at[pl.ds(p * prow, prow)]

    def flow(kind, src, dst, p, target):
        return pltpu.make_async_remote_copy(piece(src, p), piece(dst, p), send_sem.at[kind, p], recv_sem.at[kind, p], device_id=target, device_id_type=MESH)

    c_sends, c_recvs = y < ny - 1, y > 0
    f_sends, f_recvs = x < nx - 1, x > 0
    g_sends, g_recvs = jnp.logical_and(y > 0, x > 0), jnp.logical_and(y > 0, x < nx - 1)

    def comm(s):
        def at(lag):
            p = s - lag * LAG
            return p, jnp.logical_and(p >= 0, p < total)

        def arrive(live, recvs, p, ref, copy):
            @pl.when(jnp.logical_and(live, recvs))
            def _():
                copy.wait_recv()

            @pl.when(jnp.logical_and(live, jnp.logical_not(recvs)))
            def _():
                ref[pl.ds(p * prow, prow)] = jnp.zeros((prow, 8, head_v), F32)

        p, live = at(y)
        arrive(live, c_recvs, p, c_in, flow(0, c_out, c_in, p, down))

        @pl.when(jnp.logical_and(live, c_sends))
        def _(p=p):
            h = lax.div(p, PIECES)
            at_p = pl.ds(p * prow, prow)
            c_out[at_p] = coef[3, h] * c_in[at_p] + coef[2, h] * state[at_p]
            flow(0, c_out, c_in, p, down).start()

        p, live = at(y + x)
        arrive(live, f_recvs, p, f_in, flow(1, f_out, f_in, p, right))

        @pl.when(jnp.logical_and(live, f_sends))
        def _(p=p):
            h = lax.div(p, PIECES)
            at_p = pl.ds(p * prow, prow)
            f_out[at_p] = coef[0, h] * (f_in[at_p] + coef[1, h] * c_in[at_p]) + state[at_p]
            flow(1, f_out, f_in, p, right).start()

        p, live = at(y + nx - 1 - x)
        arrive(live, g_recvs, p, g_in, flow(2, g_out, g_in, p, left))

        @pl.when(jnp.logical_and(live, g_sends))
        def _(p=p):
            at_p = pl.ds(p * prow, prow)
            g_out[at_p] = g_in[at_p] + c_in[at_p]
            flow(2, g_out, g_in, p, left).start()

        p, live = at(y + jnp.maximum(x, nx - 1 - x))

        @pl.when(live)
        def _(p=p):
            h = lax.div(p, PIECES)
            at_p = pl.ds(p * prow, prow)
            state[at_p] = f_in[at_p] + coef[1, h] * (c_in[at_p] + g_in[at_p])

    def score_block(h, b, src):
        same = src == b
        q = proj[n_heads + h, b, :, 0:head_k]
        keys = proj[h, src, :, 0:head_k]
        score = lax.dot_general(q, keys, (((1,), (1,)), ((), ())), preferred_element_type=F32)
        cum_i = column(cl, b, h)
        cum_j = row_of(src, h)
        rest = jnp.where(same, -cum_j, cum_j[:, rows - 1:rows] - cum_j)
        ahead = lax.broadcasted_iota(jnp.int32, (rows, rows), 1) - lax.broadcasted_iota(jnp.int32, (rows, rows), 0)
        causal = ahead <= jnp.where(same, 0, rows)
        weight = jnp.where(causal, jnp.exp(jnp.where(causal, cum_i + rest, 0.0)), 0.0)
        vals = proj[h, src, :, head_k:blk].astype(F32)
        part = jnp.dot(score * weight, vals, preferred_element_type=F32)
        intra[h, b] = jnp.where(src == 0, 0.0, intra[h, b]) + part

    nrow = 64
    scale = head_k ** -0.5

    def finish_half(h, b):
        q = proj[n_heads + h, b, :, 0:head_k].astype(F32)
        entering = state[pl.ds(h * hrow, hrow)].reshape(head_k, head_v)
        inter = jnp.dot(q, entering, preferred_element_type=F32) * column(ecum, b, h)
        intra[h, b] = (intra[h, b] + inter) * scale
        gain = norm_w[0:1, pl.ds(pl.multiple_of(h * head_v, 128), head_v)]

        def norm(i, carry):
            at_r = pl.ds(pl.multiple_of(i * nrow, nrow), nrow)
            o = intra[h, b, at_r, :]
            z = proj[n_heads + h, b, at_r, head_k:blk].astype(F32)
            n = o * lax.rsqrt(jnp.mean(o * o, axis=1, keepdims=True) + NORM_EPS) * gain
            y_v[at_r, :] = (n * (z / (1.0 + jnp.exp(-z)))).astype(BF16)
            return carry
        lax.fori_loop(0, rows // nrow, norm, 0)

        def project(j, carry):
            cols = pl.ds(pl.multiple_of(j * head_v, 128), head_v)
            part = jnp.dot(y_v[...], wo_v[lax.rem(h, 2), :, cols], preferred_element_type=F32)
            new = jnp.where(h > 0, acc[b, :, cols], 0.0) + part
            acc[b, :, cols] = new
            x_v[b, :, cols] = new.astype(BF16)
            return carry
        lax.fori_loop(0, w_out.shape[1] // head_v, project, 0)

    o_send = pltpu.make_async_remote_copy(x_v.at[1 - core], out.at[core], os_sem, or_sem, device_id=partner, device_id_type=MESH)
    o_store = pltpu.make_async_copy(x_v.at[core], out.at[core], o_sem)

    per = 2 * tiles
    at_state, at_qz = per, per + 1
    at_score = at_qz + per
    at_fin = at_score + 3
    first_fins = 2 * (n_heads - 2)
    ends = at_fin + first_fins
    lags = (ny - 1 + nx - 1) * LAG
    last = n_heads - 1

    def slot_body(r, u):
        start = r == 0
        fin_round = r >= n_heads

        @pl.when(jnp.logical_and(start, u == 0))
        def _():
            x_load.wait()

        @pl.when(jnp.logical_and(start, u == tiles))
        def _():
            x_recv.wait_recv()

        @pl.when(jnp.logical_and(start, jnp.logical_or(u == 0, u == tiles)))
        def _():
            gate_half(jnp.where(u == 0, core, 1 - core))

        @pl.when(jnp.logical_and(start, u == tiles))
        def _():
            chip_decays()

        @pl.when(u == 0)
        def _():
            w_wait(kv_seq(r), True, r)

        @pl.when(u == at_qz)
        def _():
            w_wait(qz_seq(r - 1), False, r - 1)

        is_kv = u < at_state

        @pl.when(jnp.logical_or(is_kv, jnp.logical_and(u >= at_qz, u < at_score)))
        def _():
            v = jnp.where(is_kv, u, u - at_qz)
            b = jnp.where(v < tiles, core, 1 - core)
            seq = jnp.where(is_kv, kv_seq(r), qz_seq(r - 1))
            proj_half(seq, jnp.where(is_kv, r, n_heads + r - 1), lax.rem(v, tiles), b)

        @pl.when(u == at_state)
        def _():
            fetch_kv = start
            w_start(jnp.where(fetch_kv, kv_seq(2), qz_seq(r)), fetch_kv, jnp.where(fetch_kv, 2, r))
            chip_state(r)

        @pl.when(jnp.logical_and(start, u == at_state))
        def _():
            row_weights()

        @pl.when(jnp.logical_and(r == 1, u == at_score))
        def _():
            w_start(kv_seq(3), True, 3)
            wo_copy(0).start()
            wo_copy(1).start()

        @pl.when(jnp.logical_and(u >= at_score, u < at_fin))
        def _():
            v = u - at_score
            score_block(r - 1, jnp.where(v == 0, 0, 1), jnp.where(v == 2, 1, 0))

        @pl.when(u >= at_fin)
        def _():
            v = u - at_fin
            h = jnp.where(r == n_heads, lax.div(v, 2), r - 3)
            second = lax.rem(v, 2)

            @pl.when(second == 0)
            def _():
                wo_copy(h).wait()
            finish_half(h, jnp.where(second == 0, 1 - core, core))

            @pl.when(jnp.logical_and(second == 1, h + 2 < n_heads))
            def _():
                wo_copy(h + 2).start()

            @pl.when(jnp.logical_and(second == 0, h == last))
            def _():
                o_send.start()

            @pl.when(jnp.logical_and(second == 1, h == last))
            def _():
                o_store.start()

        early = (r - 1) * at_fin + u
        v = u - at_qz
        mid_slots = ends - at_qz
        w = u - (ends - 2)
        base = last * PIECES
        begin = jnp.where(r < n_heads, lax.div(early * PIECES, at_fin),
                          jnp.where(r == n_heads, base + lax.div(v * lags, mid_slots), base + lags + lax.div(w * PIECES, 4)))
        stop = jnp.where(r < n_heads, lax.div((early + 1) * PIECES, at_fin),
                         jnp.where(r == n_heads, base + lax.div((v + 1) * lags, mid_slots),
                                   base + lags + jnp.where(w == 0, PIECES // 4, PIECES)))
        live = jnp.logical_and(r > 0, r < n_heads + 2)

        def step(s, c):
            comm(s)
            return c
        lax.fori_loop(jnp.where(live, begin, 0), jnp.where(live, stop, 0), step, 0)

    def round_body(r, carry):
        lo = jnp.where(r < n_heads, 0, jnp.where(r == n_heads, at_qz, ends - 2))
        hi = jnp.where(r == 0, at_qz, jnp.where(r < n_heads, at_fin, ends))

        def one(u, c):
            slot_body(r, u)
            return c
        lax.fori_loop(lo, hi, one, 0)
        return carry
    lax.fori_loop(0, n_heads + 3, round_body, 0)

    x_send.wait_send()
    for o in range(1, nx):
        d_copy(o, x).wait_send()

    def drain(p, c):
        @pl.when(c_sends)
        def _():
            flow(0, c_out, c_in, p, down).wait_send()

        @pl.when(f_sends)
        def _():
            flow(1, f_out, f_in, p, right).wait_send()

        @pl.when(g_sends)
        def _():
            flow(2, g_out, g_in, p, left).wait_send()
        return c
    lax.fori_loop(0, total, drain, 0)
    o_store.wait()
    o_send.wait_send()
    pltpu.make_async_remote_copy(x_v.at[1 - core], out.at[1 - core], os_sem, or_sem, device_id=partner, device_id_type=MESH).wait_recv()


def solution(mesh):
    ny, nx = chip_grid(mesh.shape['sp'] // CORES)

    def device_body(hidden, w_in, w_gate, gate_bias, a_log, norm_w, w_out):
        _, rows, d_model = hidden.shape
        n_heads = w_gate.shape[1]
        val_dim = w_out.shape[0]
        key_dim = (w_in.shape[1] - 2 * val_dim) // 2
        head_k, head_v = key_dim // n_heads, val_dim // n_heads
        blk = head_k + head_v
        total = n_heads * PIECES
        any_space = pl.BlockSpec(memory_space=pl.ANY)
        vmem = pl.BlockSpec(memory_space=pltpu.VMEM)
        flow_buf = pltpu.VMEM((n_heads * head_k // 8, 8, head_v), F32)
        dma = pltpu.SemaphoreType.DMA
        return pl.pallas_call(
            functools.partial(layer_kernel, ny, nx),
            out_shape=jax.ShapeDtypeStruct(hidden.shape, BF16),
            in_specs=[any_space, any_space, vmem, vmem, vmem, vmem, any_space],
            out_specs=any_space,
            scratch_shapes=[
                pltpu.VMEM((2, rows, d_model), BF16),
                pltpu.VMEM((3, d_model, blk), BF16),
                pltpu.VMEM((2, head_v, w_out.shape[1]), BF16),
                pltpu.VMEM((128, d_model), BF16),
                pltpu.VMEM((16, 128), F32),
                pltpu.VMEM((2 * n_heads, 2, rows, blk), BF16),
                pltpu.VMEM((n_heads, 2, rows, head_v), F32),
                pltpu.VMEM((2, rows, w_out.shape[1]), F32),
                pltpu.VMEM((rows, head_v), BF16),
                pltpu.VMEM((2, rows, 128), F32),
                pltpu.VMEM((2, 128, rows), F32),
                pltpu.VMEM((2, rows, 128), F32),
                pltpu.VMEM((2, rows, 128), F32),
                pltpu.VMEM((8, 128), F32),
                pltpu.VMEM((nx, 8, 128), F32),
                pltpu.VMEM((4, n_heads, 8, head_v), F32),
                flow_buf, flow_buf, flow_buf, flow_buf, flow_buf, flow_buf, flow_buf,
                dma, dma, dma, dma((3, 2)), dma((2,)), dma((nx - 1,)), dma((nx - 1,)),
                dma((3, total)), dma((3, total)), dma, dma, dma,
            ],
            compiler_params=pltpu.CompilerParams(collective_id=0, has_side_effects=True, vmem_limit_bytes=67043328),
        )(hidden, w_in, w_gate.T, gate_bias.reshape(1, -1), a_log.reshape(1, -1), norm_w.reshape(1, -1), w_out)

    return jax.shard_map(device_body, mesh=mesh, in_specs=(P('dp', 'sp', None), P(), P(), P(), P(), P(), P()), out_specs=P('dp', 'sp', None), check_vma=False)
```

time: 108 us -> 99 us (0.917)
  Pallas kernels: 102 us -> 94.9 us
  local copies, waits for them, and re-layouts: 5.74 us -> 3.97 us
    pallas_call x1, Pallas kernels: 102 us -> 94.9 us  [device_body(): pl.pallas_call(functools.partial(layer_kernel, ny, nx), out_shape=jax.Sha...]
    unnamed x2 -> x1, local copies, waits for them, and re-layouts: 5.74 us -> 3.97 us
where the time goes in v2:
time: 99 us; the launch traced here: 98.9 us
  Pallas kernels  94.9 us (96%)
  local copies, waits for them, and re-layouts  3.97 us (4%)
    pallas_call x1, Pallas kernels, device_body(): pl.pallas_call(functools.partial(layer_kernel, ny, nx), out_shape=jax.Sha...  94.9 us
    unnamed x1, local copies, waits for them, and re-layouts  3.97 us

profile of v2, /device:TPU:120, one launch (start us, length us, event | category | flops | bytes accessed | tf_op | source)
XLA Modules:
  0.0 98.9 jit_solution(13503073046411732815)
XLA Ops:
  0.0 94.9 %shard_map.73 = bf16[2,384,2048]{2,1,0:T(8,128)(2,1)} custom-call(bf16[2,384,2048]{2,1,0:T(8,128)(2,1)} %hidden.1, bf16[2048,6144]{1,0:T(8,128)(2,1)} %w_in.1, bf16[4,2048]{1,0:T(4,128)(2,1)} %bitcast.4, f32[1,4]{1,0:T(1,128)} %bitcast.6, f32[1,4]{1,0:T(1,128)} %bitcast.7, f32[1,2048]{1,0:T(1,128)} %bitcast.5, bf16[2048,2048]{1,0:T(8,128)(2,1)} %w_out.1), custom_call_target="tpu_custom_call" | custom-call | tf_op jit(solution)/shard_map/pallas_call | solution.py:452
  94.9 4.0 %copy.9 = bf16[2,384,2048]{2,1,0:T(8,128)(2,1)} copy(bf16[2,384,2048]{2,1,0:T(8,128)(2,1)} %shard_map.73) | data formatting | bytes 6291456
